TPU v7x, 32 devices: a whole 2x2x4 slice. The times are simulated.
32 devices in a mesh: ep: 4 (over y, x), fsdp: 8 (over z, core).
Axes of the slice: x: 2, y: 2, z: 4, core: 2. Of those that a mesh axis runs over, the one named last changes fastest.
Arguments:
- master_down: float32 [16, 6400, 4096], P('ep', None, 'fsdp'), may hold values from -0.109375 to 0.109375
- second_down: bfloat16 [16, 6400, 4096], P('ep', None, 'fsdp'), may hold values from -0.0390625 to 0.0390625
- router_weight: float32 [4096, 16], P('fsdp', 'ep'), may hold values from -0.09375 to 0.09375
- router_gain: float32 [4096], P('fsdp'), may hold values from 0.25 to 1.75
Outputs:
- final_down: bfloat16 [16, 6400, 4096], P('ep', 'fsdp')
- scale_down: float32 [16, 6400], P('ep', 'fsdp')
- serve_router: bfloat16 [4096, 16], replicated
All inputs are finite; a program needn't handle non-finite values. Where the computation divides by a largest or mean magnitude, that divisor is 1e-20 or more.
Results may differ from a plain program's by a relative error of at most 0.001.
Values may be sent and summed in bfloat16 or wider, within the bound.
A program may use at most 256 MiB of HBM per device.

v0:
```python
import jax
import jax.numpy as jnp
from jax import lax
from jax.sharding import PartitionSpec as P


def on_device(master_down, second_down, router_weight, router_gain):
    merged_down = master_down + second_down.astype(jnp.float32)
    scale_down = lax.pmax(jnp.max(jnp.abs(merged_down), axis=2), "fsdp")
    narrow_down = (merged_down / jnp.expand_dims(scale_down, 2)).astype(jnp.bfloat16)
    final_down = lax.all_to_all(narrow_down, "fsdp", split_axis=1, concat_axis=2, tiled=True)
    scale_down = lax.dynamic_slice_in_dim(
        scale_down, lax.axis_index("fsdp") * final_down.shape[1], final_down.shape[1], axis=1
    )
    part_router = (router_weight * router_gain[:, None]).astype(jnp.bfloat16)
    row_router = lax.all_gather(part_router, "fsdp", axis=0, tiled=True)
    serve_router = lax.all_gather(row_router, "ep", axis=1, tiled=True)
    return (final_down, scale_down, serve_router)


def solution(mesh):
    placed = (P("ep", None, "fsdp"), P("ep", None, "fsdp"), P("fsdp", "ep"), P("fsdp"))
    return jax.shard_map(
        on_device,
        mesh=mesh,
        in_specs=placed,
        out_specs=(P("ep", "fsdp", None), P("ep", "fsdp"), P()),
        check_vma=False,
    )
```

profile of v0, /device:TPU:9, one launch (start us, length us, event | category | flops | bytes accessed | tf_op | source)
XLA Modules:
  0.0 835.9 jit_solution(15545822426802912631)
XLA Ops:
  7.2 0.0 all-reduce.2.cloned.1.call-start
  7.2 24.2 %abs_reduce_fusion = f32[4,6400]{1,0:T(4,128)S(1)} fusion(f32[4,6400,512]{2,1,0:T(8,128)} %param.4, bf16[4,6400,512]{2,1,0:T(8,128)(2,1)} %param.5), kind=kLoop, calls=%fused_computation.1 | loop fusion | flops 52403200 | bytes 78745600 | tf_op jit(solution)/shard_map/reduce_max | solution.py:9
  31.4 2.3 copy.21
  33.7 0.0 all-reduce.2.cloned.1.call-update
  33.7 80.3 %all-reduce.2.cloned.1.call-done = f32[4,6400]{0,1:T(8,128)} async-done(((f32[4,6400]{0,1:T(8,128)}), f32[4,6400]{0,1:T(8,128)}) %all-reduce.2.cloned.1.call-update) | async-done | bytes 102416 | tf_op jit(solution)/shard_map/pmax | solution.py:9
  114.0 2.4 copy.17
  116.5 34.3 %divide_convert_fusion = bf16[4,6400,512]{2,1,0:T(8,128)(2,1)} fusion(f32[4,6400,512]{2,1,0:T(8,128)} %param.4, bf16[4,6400,512]{2,1,0:T(8,128)(2,1)} %param.5, f32[4,6400]{1,0:T(4,128)S(1)} %copy.17), kind=kLoop, calls=%fused_computation | loop fusion | flops 52428800 | bytes 104960000 | tf_op jit(solution)/shard_map/convert_element_type | solution.py:10
  150.8 33.4 %copy.18 = bf16[4,6400,512]{2,0,1:T(4,128)(2,1)} copy(bf16[4,6400,512]{2,1,0:T(8,128)(2,1)} %divide_convert_fusion) | data formatting | bytes 52428800 | tf_op jit(solution)/shard_map/convert_element_type | solution.py:10
  184.1 0.0 copy-start
  184.1 0.0 copy-start.1
  184.2 7.6 all-to-all-start
  191.7 0.0 copy-done
  191.7 0.0 copy-done.1
  191.7 571.0 %all_gather.6 = bf16[4096,4]{0,1:T(4,128)(2,1)S(1)} all-gather(bf16[512,4]{0,1:T(4,128)(2,1)S(1)} %multiply_convert_fusion), channel_id=1, replica_groups=mesh['ep'=4,'fsdp'=8] {'fsdp'}, dimensions={0}, use_global_device_ids=true | all-gather | bytes 36864 | tf_op jit(solution)/shard_map/all_gather | solution.py:16
  762.7 6.4 all-gather
  769.1 0.7 reshape.9
  769.8 1.0 constant_dynamic-slice_fusion
  770.8 0.8 copy.20
  771.6 0.0 all-to-all-done
  771.6 18.2 %copy.19 = bf16[4,800,8,512]{3,2,1,0:T(8,128)(2,1)} copy(bf16[4,800,8,512]{3,0,1,2:T(4,128)(2,1)} %bitcast.1) | data formatting | bytes 52428800 | tf_op jit(solution)/shard_map/all_to_all | solution.py:11
  789.8 39.2 %all_to_all.16 = bf16[4,800,4096]{2,1,0:T(8,128)(2,1)} reshape(bf16[4,800,8,512]{3,2,1,0:T(8,128)(2,1)} %copy.19) | data formatting | bytes 52428800 | tf_op jit(solution)/shard_map/all_to_all | solution.py:11
  (1 shorter events, 0.0 us)
Async XLA Ops:
  7.2 106.9 %all-reduce.2.cloned.1.call-start = ((), (), s32[]{:S(2)}) async-start(), calls=%async_computation.1 | async-start | bytes 6553600 | tf_op jit(solution)/shard_map/pmax | solution.py:9
  184.1 7.6 copy-start
  184.1 7.6 copy-start.1
  184.2 587.5 %all-to-all-start = ((bf16[4,6400,512]{2,0,1:T(4,128)(2,1)}), bf16[4,6400,512]{2,0,1:T(4,128)(2,1)}, u32[]{:S(2)}, u32[]{:S(2)}) async-start(bf16[4,6400,512]{2,0,1:T(4,128)(2,1)} %copy.18), calls=%async_computation | async-start | bytes 52428800 | tf_op jit(solution)/shard_map/all_to_all | solution.py:11
Sparse Core Ops, SparseCore 0:
  33.9 80.1 all-reduce.1
where the time goes:
time: 841 us; the launch traced here: 836 us
  blocking collectives  577 us (69%)
  local copies, waits for them, and re-layouts  98 us (12%)
  waiting for transfers between devices  80.3 us (10%)
  other arithmetic  58.5 us (7%)
  between operations  14.1 us (2%)
    all_gather x1, blocking collectives, on_device(): row_router = lax.all_gather(part_router, 'fsdp', axis=0, tiled=True)  571 us
    pmax x1, waiting for transfers between devices, on_device(): scale_down = lax.pmax(jnp.max(jnp.abs(merged_down), axis=2), 'fsdp')  80.3 us
    all_to_all x2, local copies, waits for them, and re-layouts, on_device(): lax.all_to_all(narrow_down, 'fsdp', split_axis=1, concat_axis=2, tiled=True)  57.4 us
    convert_element_type x1, other arithmetic, on_device(): (merged_down / jnp.expand_dims(scale_down, 2)).astype(jnp.bfloat16)  34.3 us
    convert_element_type x1, local copies, waits for them, and re-layouts, on_device(): (merged_down / jnp.expand_dims(scale_down, 2)).astype(jnp.bfloat16)  33.4 us
    reduce_max x1, other arithmetic, on_device(): scale_down = lax.pmax(jnp.max(jnp.abs(merged_down), axis=2), 'fsdp')  24.2 us
  transfers between devices with their start and end apart: 2, of which 1 were waited for; matrix products, arithmetic and copies ran while one was open for 0% of the time, Pallas kernels for 0%

commit v1 on v0

v1 whole, which is shorter than its diff:
```python
import functools

import jax
import jax.numpy as jnp
from jax import lax
from jax.experimental import pallas as pl
from jax.experimental.pallas import tpu as pltpu
from jax.sharding import PartitionSpec as P

MESH = pl.DeviceIdType.MESH
LANES = 128
SLOTS = 3


def partner(me, step, count):
    result, bit = 0, 1
    while bit < count:
        mine, theirs = (me // bit) % 2, (step // bit) % 2
        result = result + bit * (mine + theirs - 2 * mine * theirs)
        bit *= 2
    return result


def kernel(sizes, master, second, router, gain, final, scale_out, router_out,
           wide, change, narrow, local_max, peer_max, scales, inverse, parts,
           load_sem, rs_send, rs_recv, ag_send, ag_recv, send_sem, recv_sem,
           ep_send, ep_recv, row_send, row_recv):
    experts, rows, columns, blocks, n_ep, n_fsdp = sizes
    me, group = lax.axis_index("fsdp"), lax.axis_index("ep")
    units = experts * n_fsdp

    def loads(t):
        unit, slot = t % units, t % SLOTS
        expert, owner = unit // n_fsdp, partner(me, unit % n_fsdp, n_fsdp)
        span = pl.ds(pl.multiple_of(owner * rows, 8), rows)
        return (
            pltpu.make_async_copy(
                master.at[expert, span, :], wide.at[slot, pl.ds(0, rows), :], load_sem.at[0, slot]),
            pltpu.make_async_copy(
                second.at[expert, span, :], change.at[slot, pl.ds(0, rows), :], load_sem.at[1, slot]),
        )

    def start_loads(t):
        for copy in loads(t):
            copy.start()

    def wait_loads(t):
        for copy in loads(t):
            copy.wait()

    def to_fsdp(source, target, send, recv, owner):
        return pltpu.make_async_remote_copy(
            src_ref=source, dst_ref=target, send_sem=send, recv_sem=recv,
            device_id={"fsdp": owner}, device_id_type=MESH)

    def max_copy(expert, step):
        owner = partner(me, step, n_fsdp)
        return to_fsdp(local_max.at[owner, expert], peer_max.at[step, expert],
                       rs_send.at[expert, step], rs_recv.at[expert, step], owner)

    def scale_copy(expert, step):
        owner = partner(me, step, n_fsdp)
        return to_fsdp(scales.at[me, expert], scales.at[me, expert],
                       ag_send.at[expert, step], ag_recv.at[expert, step], owner)

    def piece_copy(expert, step):
        owner = partner(me, step, n_fsdp)
        return to_fsdp(narrow.at[expert, owner, pl.ds(0, rows), :],
                       final.at[expert, :, pl.ds(pl.multiple_of(me * columns, LANES), columns)],
                       send_sem.at[expert, step], recv_sem.at[expert, step], owner)

    def own_copy(expert):
        return pltpu.make_async_copy(
            narrow.at[expert, me, pl.ds(0, rows), :],
            final.at[expert, :, pl.ds(pl.multiple_of(me * columns, LANES), columns)],
            send_sem.at[expert, 0])

    def column_copy(step):
        return pltpu.make_async_remote_copy(
            src_ref=parts.at[me, group], dst_ref=parts.at[me, group],
            send_sem=ep_send.at[step], recv_sem=ep_recv.at[step],
            device_id={"ep": partner(group, step, n_ep)}, device_id_type=MESH)

    def row_copy(step):
        return to_fsdp(parts.at[me], parts.at[me], row_send.at[step], row_recv.at[step],
                       partner(me, step, n_fsdp))

    def over(start, stop, body):
        def run(step, carry):
            body(step)
            return carry
        lax.fori_loop(start, stop, run, 0)

    for t in range(SLOTS):
        start_loads(t)
    parts[me, group] = (router[...] * gain[...]).astype(jnp.bfloat16)
    local_max[...] = jnp.zeros_like(local_max)
    if rows < blocks * LANES:
        for slot in range(SLOTS):
            wide[slot, rows:, :] = jnp.zeros((blocks * LANES - rows, columns), jnp.float32)
            change[slot, rows:, :] = jnp.zeros((blocks * LANES - rows, columns), jnp.bfloat16)

    barrier = pltpu.get_barrier_semaphore()
    for step in range(1, n_fsdp):
        pl.semaphore_signal(barrier, inc=1, device_id={"fsdp": partner(me, step, n_fsdp)}, device_id_type=MESH)
    for step in range(1, n_ep):
        pl.semaphore_signal(barrier, inc=1, device_id={"ep": partner(group, step, n_ep)}, device_id_type=MESH)
    pl.semaphore_wait(barrier, n_fsdp + n_ep - 2)
    over(1, n_ep, lambda step: column_copy(step).start())

    def merged(slot, block):
        span = pl.ds(block * LANES, LANES)
        return wide[slot, span, :] + change[slot, span, :].astype(jnp.float32)

    def share_scales(expert):
        over(1, n_fsdp, lambda step: max_copy(expert, step).wait_recv())
        top = local_max[me, expert]
        for step in range(1, n_fsdp):
            top = jnp.maximum(top, peer_max[step, expert])
        scales[me, expert] = top
        over(1, n_fsdp, lambda step: scale_copy(expert, step).start())

    for expert in range(experts):
        def find_max(step):
            t = expert * n_fsdp + step
            wait_loads(t)
            owner, slot = partner(me, step, n_fsdp), t % SLOTS
            for block in range(blocks):
                sizes_of = jnp.abs(merged(slot, block))
                top = sizes_of[:, :LANES]
                for first in range(LANES, columns, LANES):
                    top = jnp.maximum(top, sizes_of[:, first:first + LANES])
                local_max[owner, expert, pl.ds(block, 1), :] = jnp.max(top.T, axis=0, keepdims=True)
            start_loads(t + SLOTS)

        over(0, n_fsdp, find_max)
        over(1, n_fsdp, lambda step: max_copy(expert, step).start())
        if expert == 0:
            over(1, n_ep, lambda step: column_copy(step).wait())
            over(1, n_fsdp, lambda step: row_copy(step).start())
        else:
            share_scales(expert - 1)
    share_scales(experts - 1)

    for expert in range(experts):
        over(1, n_fsdp, lambda step: scale_copy(expert, step).wait_recv())
        inverse[...] = 1.0 / scales[:, expert]

        def scale_piece(step):
            t = units + expert * n_fsdp + step
            wait_loads(t)
            owner, slot = partner(me, step, n_fsdp), t % SLOTS
            for block in range(blocks):
                row = inverse[owner, pl.ds(block, 1), :]
                factor = jnp.broadcast_to(row, (LANES, LANES)).T
                whole = merged(slot, block)
                for first in range(0, columns, LANES):
                    narrow[expert, owner, pl.ds(block * LANES, LANES), first:first + LANES] = (
                        whole[:, first:first + LANES] * factor).astype(jnp.bfloat16)

            @pl.when(t + SLOTS < 2 * units)
            def _():
                start_loads(t + SLOTS)

            @pl.when(step == 0)
            def _():
                own_copy(expert).start()

            @pl.when(step > 0)
            def _():
                piece_copy(expert, step).start()

        over(0, n_fsdp, scale_piece)

    scale_out[...] = scales[me]
    over(1, n_fsdp, lambda step: row_copy(step).wait())
    router_out[...] = parts[...]
    for expert in range(experts):
        own_copy(expert).wait()
        over(1, n_fsdp, lambda step: max_copy(expert, step).wait_send())
        over(1, n_fsdp, lambda step: scale_copy(expert, step).wait_send())
        over(1, n_fsdp, lambda step: piece_copy(expert, step).wait())


def solution(mesh):
    n_ep, n_fsdp = mesh.shape["ep"], mesh.shape["fsdp"]

    def on_device(master_down, second_down, router_weight, router_gain):
        experts, all_rows, columns = master_down.shape
        rows = all_rows // n_fsdp
        blocks = -(-rows // LANES)
        held = -(-blocks // 8) * 8
        depth, width = router_weight.shape
        dma = pltpu.SemaphoreType.DMA
        vmem, hbm = pl.BlockSpec(memory_space=pltpu.VMEM), pl.BlockSpec(memory_space=pl.ANY)
        final_down, scales, parts = pl.pallas_call(
            functools.partial(kernel, (experts, rows, columns, blocks, n_ep, n_fsdp)),
            out_shape=(
                jax.ShapeDtypeStruct((experts, rows, columns * n_fsdp), jnp.bfloat16),
                jax.ShapeDtypeStruct((experts, held, LANES), jnp.float32),
                jax.ShapeDtypeStruct((n_fsdp, n_ep, width, depth), jnp.bfloat16),
            ),
            in_specs=[hbm, hbm, vmem, vmem],
            out_specs=(hbm, vmem, vmem),
            scratch_shapes=[
                pltpu.VMEM((SLOTS, blocks * LANES, columns), jnp.float32),
                pltpu.VMEM((SLOTS, blocks * LANES, columns), jnp.bfloat16),
                pltpu.VMEM((experts, n_fsdp, blocks * LANES, columns), jnp.bfloat16),
                pltpu.VMEM((n_fsdp, experts, held, LANES), jnp.float32),
                pltpu.VMEM((n_fsdp, experts, held, LANES), jnp.float32),
                pltpu.VMEM((n_fsdp, experts, held, LANES), jnp.float32),
                pltpu.VMEM((n_fsdp, held, LANES), jnp.float32),
                pltpu.VMEM((n_fsdp, n_ep, width, depth), jnp.bfloat16),
                dma((2, SLOTS)),
                dma((experts, n_fsdp)), dma((experts, n_fsdp)),
                dma((experts, n_fsdp)), dma((experts, n_fsdp)),
                dma((experts, n_fsdp)), dma((experts, n_fsdp)),
                dma((n_ep,)), dma((n_ep,)), dma((n_fsdp,)), dma((n_fsdp,)),
            ],
            compiler_params=pltpu.CompilerParams(
                collective_id=0, has_side_effects=True, vmem_limit_bytes=60 * 1024 * 1024),
        )(master_down, second_down, router_weight.T, router_gain[None, :])
        scale_down = scales.reshape(experts, held * LANES)[:, :rows]
        serve_router = parts.transpose(0, 3, 1, 2).reshape(n_fsdp * depth, n_ep * width)
        return final_down, scale_down, serve_router

    placed = (P("ep", None, "fsdp"), P("ep", None, "fsdp"), P("fsdp", "ep"), P("fsdp"))
    return jax.shard_map(
        on_device,
        mesh=mesh,
        in_specs=placed,
        out_specs=(P("ep", "fsdp", None), P("ep", "fsdp"), P()),
        check_vma=False,
    )
```

time: 841 us -> 621 us (0.74)
  Pallas kernels: 0 us -> 600 us
  blocking collectives: 577 us -> 0 us
  waiting for transfers between devices: 80.3 us -> 0 us
  local copies, waits for them, and re-layouts: 98 us -> 20.9 us
  other arithmetic: 58.5 us -> 0 us
  between operations: 14.1 us -> 0.64 us
    pallas_call x0 -> x1, Pallas kernels: none -> 600 us  [on_device(): pl.pallas_call(functools.partial(kernel, (experts, rows, columns, blocks,...]
    all_gather x2 -> x0, blocking collectives: 577 us -> none  [the longest x1 571 us: on_device(): row_router = lax.all_gather(part_router, 'fsdp', axis=0, tiled=True)]
    pmax x1 -> x0, waiting for transfers between devices: 80.3 us -> none  [on_device(): scale_down = lax.pmax(jnp.max(jnp.abs(merged_down), axis=2), 'fsdp')]
    all_to_all x2 -> x0, local copies, waits for them, and re-layouts: 57.4 us -> none  [on_device(): lax.all_to_all(narrow_down, 'fsdp', split_axis=1, concat_axis=2, tiled=True)]
    convert_element_type x2 -> x0, other arithmetic: 34.3 us -> none  [the longest x1 34.3 us: on_device(): (merged_down / jnp.expand_dims(scale_down, 2)).astype(jnp.bfloat16)]
    convert_element_type x1 -> x0, local copies, waits for them, and re-layouts: 33.4 us -> none  [on_device(): (merged_down / jnp.expand_dims(scale_down, 2)).astype(jnp.bfloat16)]
    reduce_max x1 -> x0, other arithmetic: 24.2 us -> none  [on_device(): scale_down = lax.pmax(jnp.max(jnp.abs(merged_down), axis=2), 'fsdp')]
    unnamed x7 -> x3, local copies, waits for them, and re-layouts: 3.75 us -> 19.4 us
  transfers between devices with their start and end apart: 2 -> 0, of which waited for: 1 -> 0; matrix products, arithmetic and copies ran while one was open for 0% -> 0% of each run, Pallas kernels for 0% -> 0%
where the time goes in v1:
time: 621 us
  Pallas kernels  600 us (97%)
  local copies, waits for them, and re-layouts  20.9 us (3%)
    pallas_call x1, Pallas kernels, on_device(): pl.pallas_call(functools.partial(kernel, (experts, rows, columns, blocks,...  600 us
    unnamed x3, local copies, waits for them, and re-layouts  19.4 us

profile of v1, /device:TPU:9, one launch (start us, length us, event | category | flops | bytes accessed | tf_op | source)
XLA Modules:
  0.0 621.1 jit_solution(14089559598974754357)
XLA Ops:
  0.6 599.5 %shard_map.67 = (bf16[4,800,4096]{2,1,0:T(8,128)(2,1)}, f32[4,8,128]{2,1,0:T(8,128)}, bf16[8,4,4,512]{3,2,1,0:T(4,128)(2,1)}) custom-call(f32[4,6400,512]{2,1,0:T(8,128)} %master.1, bf16[4,6400,512]{2,1,0:T(8,128)(2,1)} %second.1, f32[4,512]{1,0:T(4,128)} %bitcast.17, f32[1,512]{1,0:T(1,128)} %bitcast.18), custom_call_target="tpu_custom_call" | custom-call | tf_op jit(solution)/shard_map/pallas_call | solution.py:196
  600.2 0.7 copy.11
  600.9 0.6 slice.4
  601.5 1.0 copy.7
  602.5 0.7 copy.9
  603.2 17.9 %copy.13 = bf16[4,800,4096]{2,1,0:T(8,128)(2,1)} copy(bf16[4,800,4096]{2,1,0:T(8,128)(2,1)} %get-tuple-element.12) | data formatting | bytes 52428800

commit v2 on v1

--- a/solution.py
+++ b/solution.py
@@ -27,11 +27,15 @@
            ep_send, ep_recv, row_send, row_recv):
     experts, rows, columns, blocks, n_ep, n_fsdp = sizes
     me, group = lax.axis_index("fsdp"), lax.axis_index("ep")
-    units = experts * n_fsdp
-
-    def loads(t):
-        unit, slot = t % units, t % SLOTS
-        expert, owner = unit // n_fsdp, partner(me, unit % n_fsdp, n_fsdp)
+    lead = min(3, experts)
+    passes = [("max", expert) for expert in range(lead)]
+    for expert in range(experts):
+        passes.append(("scale", expert))
+        if lead + expert < experts:
+            passes.append(("max", lead + expert))
+
+    def loads(t, expert, step):
+        slot, owner = t % SLOTS, partner(me, step, n_fsdp)
         span = pl.ds(pl.multiple_of(owner * rows, 8), rows)
         return (
             pltpu.make_async_copy(
@@ -40,13 +44,23 @@
                 second.at[expert, span, :], change.at[slot, pl.ds(0, rows), :], load_sem.at[1, slot]),
         )
 
-    def start_loads(t):
-        for copy in loads(t):
+    def start_loads(t, expert, step):
+        for copy in loads(t, expert, step):
             copy.start()
 
-    def wait_loads(t):
-        for copy in loads(t):
+    def wait_loads(t, expert, step):
+        for copy in loads(t, expert, step):
             copy.wait()
+
+    def load_ahead(index, step):
+        expert, ahead = passes[index][1], step + SLOTS
+        if index + 1 < len(passes):
+            later = passes[index + 1][1]
+            start_loads(index * n_fsdp + ahead, expert + (later - expert) * (ahead // n_fsdp), ahead % n_fsdp)
+        else:
+            @pl.when(ahead < n_fsdp)
+            def _():
+                start_loads(index * n_fsdp + ahead, expert, ahead)
 
     def to_fsdp(source, target, send, recv, owner):
         return pltpu.make_async_remote_copy(
@@ -92,7 +106,7 @@
         lax.fori_loop(start, stop, run, 0)
 
     for t in range(SLOTS):
-        start_loads(t)
+        start_loads(t, 0, t)
     parts[me, group] = (router[...] * gain[...]).astype(jnp.bfloat16)
     local_max[...] = jnp.zeros_like(local_max)
     if rows < blocks * LANES:
@@ -120,57 +134,54 @@
         scales[me, expert] = top
         over(1, n_fsdp, lambda step: scale_copy(expert, step).start())
 
-    for expert in range(experts):
-        def find_max(step):
-            t = expert * n_fsdp + step
-            wait_loads(t)
-            owner, slot = partner(me, step, n_fsdp), t % SLOTS
-            for block in range(blocks):
-                sizes_of = jnp.abs(merged(slot, block))
-                top = sizes_of[:, :LANES]
-                for first in range(LANES, columns, LANES):
-                    top = jnp.maximum(top, sizes_of[:, first:first + LANES])
-                local_max[owner, expert, pl.ds(block, 1), :] = jnp.max(top.T, axis=0, keepdims=True)
-            start_loads(t + SLOTS)
-
-        over(0, n_fsdp, find_max)
-        over(1, n_fsdp, lambda step: max_copy(expert, step).start())
-        if expert == 0:
-            over(1, n_ep, lambda step: column_copy(step).wait())
-            over(1, n_fsdp, lambda step: row_copy(step).start())
+    def find_max(index, expert, step):
+        t = index * n_fsdp + step
+        wait_loads(t, expert, step)
+        owner, slot = partner(me, step, n_fsdp), t % SLOTS
+        for block in range(blocks):
+            sizes_of = jnp.abs(merged(slot, block))
+            top = sizes_of[:, :LANES]
+            for first in range(LANES, columns, LANES):
+                top = jnp.maximum(top, sizes_of[:, first:first + LANES])
+            local_max[owner, expert, pl.ds(block, 1), :] = jnp.max(top.T, axis=0, keepdims=True)
+        load_ahead(index, step)
+
+    def scale_piece(index, expert, step):
+        t = index * n_fsdp + step
+        wait_loads(t, expert, step)
+        owner, slot = partner(me, step, n_fsdp), t % SLOTS
+        for block in range(blocks):
+            row = inverse[owner, pl.ds(block, 1), :]
+            factor = jnp.broadcast_to(row, (LANES, LANES)).T
+            whole = merged(slot, block)
+            for first in range(0, columns, LANES):
+                narrow[expert, owner, pl.ds(block * LANES, LANES), first:first + LANES] = (
+                    whole[:, first:first + LANES] * factor).astype(jnp.bfloat16)
+        load_ahead(index, step)
+
+        @pl.when(step == 0)
+        def _():
+            own_copy(expert).start()
+
+        @pl.when(step > 0)
+        def _():
+            piece_copy(expert, step).start()
+
+    for index, (kind, expert) in enumerate(passes):
+        if kind == "max":
+            over(0, n_fsdp, functools.partial(find_max, index, expert))
+            if expert:
+                share_scales(expert - 1)
+            over(1, n_fsdp, lambda step: max_copy(expert, step).start())
+            if expert == 0:
+                over(1, n_ep, lambda step: column_copy(step).wait())
+                over(1, n_fsdp, lambda step: row_copy(step).start())
         else:
-            share_scales(expert - 1)
-    share_scales(experts - 1)
-
-    for expert in range(experts):
-        over(1, n_fsdp, lambda step: scale_copy(expert, step).wait_recv())
-        inverse[...] = 1.0 / scales[:, expert]
-
-        def scale_piece(step):
-            t = units + expert * n_fsdp + step
-            wait_loads(t)
-            owner, slot = partner(me, step, n_fsdp), t % SLOTS
-            for block in range(blocks):
-                row = inverse[owner, pl.ds(block, 1), :]
-                factor = jnp.broadcast_to(row, (LANES, LANES)).T
-                whole = merged(slot, block)
-                for first in range(0, columns, LANES):
-                    narrow[expert, owner, pl.ds(block * LANES, LANES), first:first + LANES] = (
-                        whole[:, first:first + LANES] * factor).astype(jnp.bfloat16)
-
-            @pl.when(t + SLOTS < 2 * units)
-            def _():
-                start_loads(t + SLOTS)
-
-            @pl.when(step == 0)
-            def _():
-                own_copy(expert).start()
-
-            @pl.when(step > 0)
-            def _():
-                piece_copy(expert, step).start()
-
-        over(0, n_fsdp, scale_piece)
+            if expert == experts - lead + 1 or experts == lead == expert + 1:
+                share_scales(experts - 1)
+            over(1, n_fsdp, lambda step: scale_copy(expert, step).wait_recv())
+            inverse[...] = 1.0 / scales[:, expert]
+            over(0, n_fsdp, functools.partial(scale_piece, index, expert))
 
     scale_out[...] = scales[me]
     over(1, n_fsdp, lambda step: row_copy(step).wait())

time: 621 us -> 614 us (0.989)
  Pallas kernels: 600 us -> 592 us
    pallas_call x1, Pallas kernels: 600 us -> 592 us  [on_device(): pl.pallas_call(functools.partial(kernel, (experts, rows, columns, blocks,...]
where the time goes in v2:
time: 614 us
  Pallas kernels  592 us (96%)
  local copies, waits for them, and re-layouts  20.9 us (3%)
    pallas_call x1, Pallas kernels, on_device(): pl.pallas_call(functools.partial(kernel, (experts, rows, columns, blocks,...  592 us
    unnamed x3, local copies, waits for them, and re-layouts  19.4 us

profile of v2, /device:TPU:9, one launch (start us, length us, event | category | flops | bytes accessed | tf_op | source)
XLA Modules:
  0.0 614.0 jit_solution(15997345063815766350)
XLA Ops:
  0.6 592.4 %shard_map.67 = (bf16[4,800,4096]{2,1,0:T(8,128)(2,1)}, f32[4,8,128]{2,1,0:T(8,128)}, bf16[8,4,4,512]{3,2,1,0:T(4,128)(2,1)}) custom-call(f32[4,6400,512]{2,1,0:T(8,128)} %master.1, bf16[4,6400,512]{2,1,0:T(8,128)(2,1)} %second.1, f32[4,512]{1,0:T(4,128)} %bitcast.17, f32[1,512]{1,0:T(1,128)} %bitcast.18), custom_call_target="tpu_custom_call" | custom-call | tf_op jit(solution)/shard_map/pallas_call | solution.py:207
  593.1 0.7 copy.11
  593.8 0.6 slice.4
  594.4 1.0 copy.7
  595.4 0.7 copy.9
  596.1 17.9 %copy.13 = bf16[4,800,4096]{2,1,0:T(8,128)(2,1)} copy(bf16[4,800,4096]{2,1,0:T(8,128)(2,1)} %get-tuple-element.12) | data formatting | bytes 52428800
